TPU v7x, 32 devices: a whole 2x2x4 slice. The times are simulated.
32 devices in a mesh: cluster: 8 (over z, y), sub: 4 (over x, core).
Axes of the slice: x: 2, y: 2, z: 4, core: 2. Of those that a mesh axis runs over, the one named last changes fastest.
Arguments:
- rhs: float32 [128, 4, 384], P(('cluster', 'sub')), may hold values from -8 to 8
- operators: bfloat16 [128, 384, 384], P(('cluster', 'sub')), may hold values from -1 to 5
- signs: int32 [128, 384], P(('cluster', 'sub')), may hold values from -1 to 1, as said below
- links: int32 [128, 3, 128], P(('cluster', 'sub')), may hold values from 0 to 127, as said below
- cluster_basis: float32 [128, 24, 384], P(('cluster', 'sub')), may hold values from -0.3125 to 0.3125
- corner_basis: float32 [128, 8, 384], P(('cluster', 'sub')), may hold values from -0.3125 to 0.3125
- corner_ids: int32 [128, 8], P(('cluster', 'sub')), may hold values from 0 to 127
- cluster_coarse: float32 [8, 384, 384], P('cluster', 'sub'), may hold values from -1 to 3
- global_coarse: float32 [128, 128], P('sub'), may hold values from -0.2 to 0.5
Outputs:
- multipliers: float32 [128, 4, 384], P(('cluster', 'sub'))
- residual: float32 [128, 4, 384], P(('cluster', 'sub'))
Inputs may be any that keep to these rules, and one draw needn't show every extreme that they name: `signs`: each entry is -1 or 1. Each links[s, b] is a permutation of 0 to 127; both subdomains of an interface pair hold the same permutation for it.
All inputs are finite; a program needn't handle non-finite values.
Results may differ from a plain program's by a relative error of at most 0.007.
Values sent between devices are 32-bit elements; how exact they have to be, the bound alone decides.
A program may use at most 64 MiB of HBM per device.

v0:
```python
import jax
import jax.numpy as jnp
from jax import lax
from jax.sharding import PartitionSpec as P

ITERS = 2
HIGHEST_PRECISION = lax.Precision.HIGHEST


def extended(block, sides, width):
    for axis, dim in sides:
        count = lax.axis_size(axis)
        forward = [(i, i + 1) for i in range(count - 1)]
        backward = [(target, source) for source, target in forward]
        low = lax.ppermute(
            lax.slice_in_dim(block, block.shape[dim] - width, None, axis=dim), axis, forward
        )
        high = lax.ppermute(lax.slice_in_dim(block, 0, width, axis=dim), axis, backward)
        block = jnp.concatenate([low, block, high], axis=dim)
    return block


def invert(order):
    row_index = jnp.broadcast_to(jnp.arange(order.shape[0], dtype=jnp.int32)[:, None], order.shape)
    col_index = jnp.broadcast_to(jnp.arange(order.shape[1], dtype=jnp.int32)[None, :], order.shape)
    return jnp.zeros_like(order).at[row_index, order].set(col_index)


def permuted(blocks, order):
    return jnp.take_along_axis(blocks, order[:, None, :], axis=2)


def interface(vector, tables):
    inv_up, order_down, inv_even, order_odd = tables
    block_width = vector.shape[2] // 3
    up_part = vector[:, :, :block_width]
    down_part = vector[:, :, block_width : 2 * block_width]
    across = vector[:, :, 2 * block_width :]
    send_up = permuted(up_part, inv_up)
    send_down = permuted(down_part, order_down)
    inside_rims = extended(jnp.stack([send_down, send_up]), (("sub", 0),), 1)
    send_even = permuted(across[0::2], inv_even)
    send_odd = permuted(across[1::2], order_odd)
    outside_rims = extended(jnp.stack([send_odd, send_even]), (("cluster", 0),), 1)
    new_across = jnp.stack([outside_rims[3], outside_rims[0]], axis=1).reshape(across.shape)
    return jnp.concatenate([inside_rims[3], inside_rims[0], new_across], axis=2)


def apply(vector, sign_field, operators, tables):
    spread = sign_field * (vector + interface(vector, tables))
    product = jnp.einsum(
        "srk,skl->srl", spread.astype(jnp.bfloat16), operators, preferred_element_type=jnp.float32
    )
    curvature = lax.psum(jnp.sum(spread * product, axis=(0, 2)), ("cluster", "sub"))
    signed = sign_field * product
    result = signed + interface(signed, tables)
    return (result, curvature)


def project(vector, coarse):
    cluster_basis, corner_basis, flat_ids, onehot, cluster_coarse, global_coarse = coarse
    load_count = vector.shape[1]
    local_subs = vector.shape[0]
    cluster_coef = jnp.einsum("srl,skl->srk", vector, cluster_basis, precision=HIGHEST_PRECISION)
    own_coef = cluster_coef.transpose(1, 0, 2).reshape(load_count, -1)
    part_cluster = jnp.dot(own_coef, cluster_coarse[0], precision=HIGHEST_PRECISION)
    corner_coef = jnp.einsum(
        "scl,srl->rsc", corner_basis, vector, precision=HIGHEST_PRECISION
    ).reshape(load_count, -1)
    corner_local = jnp.dot(corner_coef, onehot, precision=HIGHEST_PRECISION)
    squares = jnp.sum(vector * vector, axis=(0, 2))
    row_count = global_coarse.shape[0]
    corner_whole, total_norm = lax.psum((corner_local, squares), ("cluster", "sub"))
    corner_rows = lax.dynamic_slice_in_dim(
        corner_whole, lax.axis_index("sub") * row_count, row_count, 1
    )
    part_global = jnp.dot(corner_rows, global_coarse, precision=HIGHEST_PRECISION)
    cluster_all, global_all = lax.psum((part_cluster, part_global), "sub")
    own_width = own_coef.shape[1]
    cluster_own = lax.dynamic_slice_in_dim(
        cluster_all, lax.axis_index("sub") * own_width, own_width, 1
    )
    cluster_own = cluster_own.reshape(load_count, local_subs, -1)
    fix_cluster = jnp.einsum(
        "rsk,skl->srl", cluster_own, cluster_basis, precision=HIGHEST_PRECISION
    )
    picked = jnp.take(global_all, flat_ids, axis=1).reshape(load_count, local_subs, -1)
    fix_corner = jnp.einsum("rsc,scl->srl", picked, corner_basis, precision=HIGHEST_PRECISION)
    return (vector - fix_cluster - fix_corner, total_norm)


def local(
    rhs,
    operators,
    signs,
    links,
    cluster_basis,
    corner_basis,
    corner_ids,
    cluster_coarse,
    global_coarse,
):
    sign_field = signs.astype(jnp.float32)[:, None, :]
    tables = (invert(links[:, 0]), links[:, 1], invert(links[0::2, 2]), links[1::2, 2])
    flat_ids = corner_ids.reshape(-1)
    onehot = (
        flat_ids[:, None] == jnp.arange(global_coarse.shape[1], dtype=jnp.int32)[None, :]
    ).astype(jnp.float32)
    coarse = (cluster_basis, corner_basis, flat_ids, onehot, cluster_coarse, global_coarse)
    residual = rhs
    projected, residual_norm = project(residual, coarse)
    direction = projected
    multipliers = jnp.zeros_like(rhs)
    for iteration in range(ITERS):
        product, curvature = apply(direction, sign_field, operators, tables)
        step_size = (residual_norm / curvature)[None, :, None]
        multipliers = multipliers + step_size * direction
        residual = residual - step_size * product
        if iteration + 1 < ITERS:
            projected, norm_next = project(residual, coarse)
            direction = projected + (norm_next / residual_norm)[None, :, None] * direction
            residual_norm = norm_next
    return (multipliers, residual)


def solution(mesh):
    placed = (
        P(("cluster", "sub"), None, None),
        P(("cluster", "sub"), None, None),
        P(("cluster", "sub"), None),
        P(("cluster", "sub"), None, None),
        P(("cluster", "sub"), None, None),
        P(("cluster", "sub"), None, None),
        P(("cluster", "sub"), None),
        P("cluster", "sub", None),
        P("sub", None),
    )
    return jax.shard_map(
        local,
        mesh=mesh,
        in_specs=placed,
        out_specs=(P(("cluster", "sub"), None, None), P(("cluster", "sub"), None, None)),
        check_vma=False,
    )
```

profile of v0, /device:TPU:1, one launch (start us, length us, event | category | flops | bytes accessed | tf_op | source)
XLA Modules:
  0.0 322.6 jit_solution(7329631267407565892)
XLA Ops:
  0.7 0.9 eq.15
  1.5 0.7 slice.78
  2.3 1.2 convolution_bitcast_fusion.3
  3.6 1.0 convolution_bitcast_fusion.2
  4.7 0.2 fusion.16
  4.9 40.5 %psum.72 = f32[4,128]{1,0:T(4,128)S(1)} all-reduce(f32[4,128]{1,0:T(4,128)S(1)} %fusion.16), channel_id=1, replica_groups=mesh['cluster'=8,'sub'=4] {'cluster','sub'}, use_global_device_ids=true, to_apply=%region_3.0 | all-reduce | flops 512 | bytes 4096 | tf_op jit(solution)/shard_map/psum | solution.py:73
  45.4 1.1 fusion.3
  46.5 0.9 fusion.46
  47.4 7.2 %all-reduce.3 = (f32[4,384]{1,0:T(4,128)S(1)}, f32[4,128]{1,0:T(4,128)S(1)}) all-reduce(f32[4,384]{1,0:T(4,128)S(1)} %fusion.3, f32[4,128]{1,0:T(4,128)S(1)} %fusion.46), channel_id=1, replica_groups=mesh['cluster'=8,'sub'=4] {'sub'}, use_global_device_ids=true, to_apply=%region_2.0 | all-reduce | flops 2048 | bytes 16384 | tf_op jit(solution)/shard_map/psum | solution.py:78
  54.8 1.1 convolution_subtract_fusion.3
  56.0 0.6 gather_fusion
  56.6 1.1 convolution_subtract_fusion.2
  57.9 1.9 gather_fusion.3
  59.9 1.3 collective-permute-start.2
  61.2 11.4 %scatter_fusion.1 = s32[2,128]{1,0:T(2,128)S(1)} fusion(s32[2,128]{1,0:T(2,128)S(1)} %broadcast.105, s32[256]{0:T(256)S(1)} %fusion.53, s32[256]{0:T(256)S(1)} %iota_bitcast_fusion.1), kind=kCustom, calls=%fused_computation.19 | custom fusion | bytes 5120 | tf_op jit(solution)/shard_map/scatter | solution.py:26
  72.9 1.9 gather_fusion.4
  74.9 4.0 %collective-permute-start.3 = (f32[1,2,4,128]{3,2,1,0:T(4,128)S(1)}, f32[1,2,4,128]{3,2,1,0:T(4,128)S(1)}, u32[]{:S(2)}, u32[]{:S(2)}) collective-permute-start(f32[1,2,4,128]{3,2,1,0:T(4,128)S(1)} %select_bitcast_fusion.6), channel_id=1, source_target_pairs={{0,4},{4,8},{8,12},{12,16},{16,20},{20,24},{24,28},{1,5},{5,9},{9,... | collective-permute-start | bytes 12296 | tf_op jit(solution)/shard_map/ppermute | solution.py:15
  79.0 3.7 %gather_fusion.1 = f32[512,4]{1,0:T(8,128)S(1)} fusion(f32[4,4,128]{1,2,0:T(8,128)S(1)} %copy.49, s32[512]{0:T(512)S(1)} %get-tuple-element.39), kind=kCustom, calls=%fused_computation.1.clone | custom fusion | bytes 20480 | tf_op jit(solution)/shard_map/jit(take_along_axis)/gather | solution.py:30
  82.8 3.1 collective-permute-start
  86.0 22.5 %scatter_fusion = s32[4,128]{1,0:T(4,128)S(1)} fusion(s32[4,128]{1,0:T(4,128)S(1)} %broadcast.103, s32[512]{0:T(512)S(1)} %get-tuple-element.40, s32[512]{0:T(512)S(1)} %iota_bitcast_fusion), kind=kCustom, calls=%fused_computation.18 | custom fusion | bytes 10240 | tf_op jit(solution)/shard_map/scatter | solution.py:26
  108.7 3.7 %gather_fusion.2 = f32[512,4]{1,0:T(8,128)S(1)} fusion(f32[4,4,128]{1,2,0:T(8,128)S(1)} %copy.51, s32[512]{0:T(512)S(1)} %fusion.40), kind=kCustom, calls=%fused_computation.4.clone | custom fusion | bytes 20480 | tf_op jit(solution)/shard_map/jit(take_along_axis)/gather | solution.py:30
  112.5 3.3 %collective-permute-start.1 = (f32[1,4,4,128]{3,2,1,0:T(4,128)S(1)}, f32[1,4,4,128]{3,2,1,0:T(4,128)S(1)}, u32[]{:S(2)}, u32[]{:S(2)}) collective-permute-start(f32[1,4,4,128]{3,2,1,0:T(4,128)S(1)} %fusion.27), channel_id=1, source_target_pairs={{0,1},{1,2},{2,3},{4,5},{5,6},{6,7},{8,9},{9,10},{10,11},{12,13},{... | collective-permute-start | bytes 24584 | tf_op jit(solution)/shard_map/ppermute | solution.py:15
  116.0 0.6 collective-permute-done.1
  116.6 0.4 multiply_reduce_fusion.2
  117.2 1.9 gather_fusion.7
  119.1 1.3 collective-permute-start.6
  120.6 1.9 gather_fusion.8
  122.6 4.4 %collective-permute-start.7 = (f32[1,2,4,128]{3,2,1,0:T(4,128)S(1)}, f32[1,2,4,128]{3,2,1,0:T(4,128)S(1)}, u32[]{:S(2)}, u32[]{:S(2)}) collective-permute-start(f32[1,2,4,128]{3,2,1,0:T(4,128)S(1)} %select_bitcast_fusion.4), channel_id=1, source_target_pairs={{0,4},{4,8},{8,12},{12,16},{16,20},{20,24},{24,28},{1,5},{5,9},{9,... | collective-permute-start | bytes 12296 | tf_op jit(solution)/shard_map/ppermute | solution.py:15
  127.2 3.7 %gather_fusion.5 = f32[512,4]{1,0:T(8,128)S(1)} fusion(f32[4,4,128]{1,2,0:T(8,128)S(1)} %copy.57, s32[512]{0:T(512)S(1)} %get-tuple-element.39), kind=kCustom, calls=%fused_computation.5.clone | custom fusion | bytes 20480 | tf_op jit(solution)/shard_map/jit(take_along_axis)/gather | solution.py:30
  131.0 2.4 collective-permute-start.4
  133.5 3.7 %gather_fusion.6 = f32[512,4]{1,0:T(8,128)S(1)} fusion(f32[4,4,128]{1,2,0:T(8,128)S(1)} %copy.59, s32[512]{0:T(512)S(1)} %fusion.40), kind=kCustom, calls=%fused_computation.6.clone | custom fusion | bytes 20480 | tf_op jit(solution)/shard_map/jit(take_along_axis)/gather | solution.py:30
  137.3 4.2 %collective-permute-start.5 = (f32[1,4,4,128]{3,2,1,0:T(4,128)S(1)}, f32[1,4,4,128]{3,2,1,0:T(4,128)S(1)}, u32[]{:S(2)}, u32[]{:S(2)}) collective-permute-start(f32[1,4,4,128]{3,2,1,0:T(4,128)S(1)} %fusion.25), channel_id=1, source_target_pairs={{0,1},{1,2},{2,3},{4,5},{5,6},{6,7},{8,9},{9,10},{10,11},{12,13},{... | collective-permute-start | bytes 24584 | tf_op jit(solution)/shard_map/ppermute | solution.py:15
  141.5 39.1 %all-reduce.1 = (f32[4]{0:T(128)S(1)}, f32[4]{0:T(128)S(1)}) all-reduce(f32[4]{0:T(128)S(1)} %multiply_reduce_fusion.3, f32[4]{0:T(128)S(1)} %get-tuple-element.17), channel_id=1, replica_groups=mesh['cluster'=8,'sub'=4] {'cluster','sub'}, use_global_device_ids=true, to_apply=%region_1.0 | all-reduce | flops 8 | bytes 64 | tf_op jit(solution)/shard_map/psum | solution.py:73
  180.7 0.2 multiply_reduce_fusion.1
  181.1 0.3 convolution_bitcast_fusion.1
  181.5 0.2 fusion.15
  181.7 38.6 %all-reduce = (f32[4,128]{1,0:T(4,128)S(1)}, f32[4]{0:T(128)S(1)}) all-reduce(f32[4,128]{1,0:T(4,128)S(1)} %fusion.15, f32[4]{0:T(128)S(1)} %get-tuple-element.13), channel_id=1, replica_groups=mesh['cluster'=8,'sub'=4] {'cluster','sub'}, use_global_device_ids=true, to_apply=%region_12.16 | all-reduce | flops 516 | bytes 4128 | tf_op jit(solution)/shard_map/psum | solution.py:73
  220.3 0.2 fusion.44
  220.6 0.2 fusion.1
  220.8 7.2 %all-reduce.2 = (f32[4,384]{1,0:T(4,128)S(1)}, f32[4,128]{1,0:T(4,128)S(1)}) all-reduce(f32[4,384]{1,0:T(4,128)S(1)} %fusion.1, f32[4,128]{1,0:T(4,128)S(1)} %fusion.44), channel_id=1, replica_groups=mesh['cluster'=8,'sub'=4] {'sub'}, use_global_device_ids=true, to_apply=%region_11.15 | all-reduce | flops 2048 | bytes 16384 | tf_op jit(solution)/shard_map/psum | solution.py:78
  228.2 0.2 convolution_subtract_fusion.1
  228.5 0.6 gather_fusion.9
  229.1 0.3 fusion
  229.6 1.9 gather_fusion.12
  231.6 1.3 collective-permute-start.10
  233.0 1.9 gather_fusion.13
  235.0 4.1 %collective-permute-start.11 = (f32[1,2,4,128]{3,2,1,0:T(4,128)S(1)}, f32[1,2,4,128]{3,2,1,0:T(4,128)S(1)}, u32[]{:S(2)}, u32[]{:S(2)}) collective-permute-start(f32[1,2,4,128]{3,2,1,0:T(4,128)S(1)} %select_bitcast_fusion.2), channel_id=1, source_target_pairs={{0,4},{4,8},{8,12},{12,16},{16,20},{20,24},{24,28},{1,5},{5,9},{9,... | collective-permute-start | bytes 12296 | tf_op jit(solution)/shard_map/ppermute | solution.py:15
  239.3 3.7 %gather_fusion.10 = f32[512,4]{1,0:T(8,128)S(1)} fusion(f32[4,4,128]{1,2,0:T(8,128)S(1)} %copy.71, s32[512]{0:T(512)S(1)} %get-tuple-element.39), kind=kCustom, calls=%fused_computation.7.clone | custom fusion | bytes 20480 | tf_op jit(solution)/shard_map/jit(take_along_axis)/gather | solution.py:30
  243.1 3.7 %collective-permute-start.8 = (f32[1,4,4,128]{3,2,1,0:T(4,128)S(1)}, f32[1,4,4,128]{3,2,1,0:T(4,128)S(1)}, u32[]{:S(2)}, u32[]{:S(2)}) collective-permute-start(f32[1,4,4,128]{3,2,1,0:T(4,128)S(1)} %fusion.24), channel_id=1, source_target_pairs={{1,0},{2,1},{3,2},{5,4},{6,5},{7,6},{9,8},{10,9},{11,10},{13,12},{... | collective-permute-start | bytes 24584 | tf_op jit(solution)/shard_map/ppermute | solution.py:18
  246.9 3.7 %gather_fusion.11 = f32[512,4]{1,0:T(8,128)S(1)} fusion(f32[4,4,128]{1,2,0:T(8,128)S(1)} %copy.73, s32[512]{0:T(512)S(1)} %fusion.40), kind=kCustom, calls=%fused_computation.8.clone | custom fusion | bytes 20480 | tf_op jit(solution)/shard_map/jit(take_along_axis)/gather | solution.py:30
  250.7 2.6 collective-permute-start.9
  253.3 0.7 collective-permute-done.9
  254.1 0.4 broadcast_multiply_fusion
  254.5 41.2 %psum.79 = f32[4]{0:T(128)S(1)} all-reduce(f32[4]{0:T(128)S(1)} %get-tuple-element.16), channel_id=1, replica_groups=mesh['cluster'=8,'sub'=4] {'cluster','sub'}, use_global_device_ids=true, to_apply=%region_15.19 | all-reduce | flops 4 | bytes 32 | tf_op jit(solution)/shard_map/psum | solution.py:54
  295.8 1.9 gather_fusion.16
  297.8 1.5 collective-permute-start.14
  299.5 1.9 gather_fusion.17
  301.4 4.0 %collective-permute-start.15 = (f32[1,2,4,128]{3,2,1,0:T(4,128)S(1)}, f32[1,2,4,128]{3,2,1,0:T(4,128)S(1)}, u32[]{:S(2)}, u32[]{:S(2)}) collective-permute-start(f32[1,2,4,128]{3,2,1,0:T(4,128)S(1)} %select_bitcast_fusion), channel_id=1, source_target_pairs={{0,4},{4,8},{8,12},{12,16},{16,20},{20,24},{24,28},{1,5},{5,9},{9,... | collective-permute-start | bytes 12296 | tf_op jit(solution)/shard_map/ppermute | solution.py:15
  305.6 3.7 %gather_fusion.14 = f32[512,4]{1,0:T(8,128)S(1)} fusion(f32[4,4,128]{1,2,0:T(8,128)S(1)} %copy.79, s32[512]{0:T(512)S(1)} %get-tuple-element.39), kind=kCustom, calls=%fused_computation.9.clone | custom fusion | bytes 20480 | tf_op jit(solution)/shard_map/jit(take_along_axis)/gather | solution.py:30
  309.4 4.2 %collective-permute-start.12 = (f32[1,4,4,128]{3,2,1,0:T(4,128)S(1)}, f32[1,4,4,128]{3,2,1,0:T(4,128)S(1)}, u32[]{:S(2)}, u32[]{:S(2)}) collective-permute-start(f32[1,4,4,128]{3,2,1,0:T(4,128)S(1)} %fusion.22), channel_id=1, source_target_pairs={{1,0},{2,1},{3,2},{5,4},{6,5},{7,6},{9,8},{10,9},{11,10},{13,12},{... | collective-permute-start | bytes 24584 | tf_op jit(solution)/shard_map/ppermute | solution.py:18
  313.8 3.7 %gather_fusion.15 = f32[512,4]{1,0:T(8,128)S(1)} fusion(f32[4,4,128]{1,2,0:T(8,128)S(1)} %copy.81, s32[512]{0:T(512)S(1)} %fusion.40), kind=kCustom, calls=%fused_computation.10.clone | custom fusion | bytes 20480 | tf_op jit(solution)/shard_map/jit(take_along_axis)/gather | solution.py:30
  317.5 3.5 %collective-permute-start.13 = (f32[1,4,4,128]{3,2,1,0:T(4,128)S(1)}, f32[1,4,4,128]{3,2,1,0:T(4,128)S(1)}, u32[]{:S(2)}, u32[]{:S(2)}) collective-permute-start(f32[1,4,4,128]{3,2,1,0:T(4,128)S(1)} %fusion.21), channel_id=1, source_target_pairs={{0,1},{1,2},{2,3},{4,5},{5,6},{6,7},{8,9},{9,10},{10,11},{12,13},{... | collective-permute-start | bytes 24584 | tf_op jit(solution)/shard_map/ppermute | solution.py:15
  321.1 0.7 collective-permute-done.13
  321.9 0.7 fusion.10
  (126 shorter events, 5.4 us)
Async XLA Ops:
  0.6 116.0 %copy-start = (bf16[4,384,384]{2,1,0:T(8,128)(2,1)S(1)}, bf16[4,384,384]{2,1,0:T(8,128)(2,1)}, u32[]{:S(2)}) copy-start(bf16[4,384,384]{2,1,0:T(8,128)(2,1)} %param.16) | copy-start | bytes 3538948
  0.6 60.5 %copy-start.6 = (s32[4,3,128]{2,0,1:T(4,128)S(1)}, s32[4,3,128]{2,0,1:T(4,128)}, u32[]{:S(2)}) copy-start(s32[4,3,128]{2,0,1:T(4,128)} %param.18) | copy-start | bytes 18436
  59.9 56.1 %collective-permute-start.2 = (f32[1,2,4,128]{3,2,1,0:T(4,128)S(1)}, f32[1,2,4,128]{3,2,1,0:T(4,128)S(1)}, u32[]{:S(2)}, u32[]{:S(2)}) collective-permute-start(f32[1,2,4,128]{3,2,1,0:T(4,128)S(1)} %select_bitcast_fusion.7), channel_id=1, source_target_pairs={{4,0},{8,4},{12,8},{16,12},{20,16},{24,20},{28,24},{5,1},{9,5},{13... | collective-permute-start | bytes 12296 | tf_op jit(solution)/shard_map/ppermute | solution.py:18
  74.9 41.1 %collective-permute-start.3 = (f32[1,2,4,128]{3,2,1,0:T(4,128)S(1)}, f32[1,2,4,128]{3,2,1,0:T(4,128)S(1)}, u32[]{:S(2)}, u32[]{:S(2)}) collective-permute-start(f32[1,2,4,128]{3,2,1,0:T(4,128)S(1)} %select_bitcast_fusion.6), channel_id=1, source_target_pairs={{0,4},{4,8},{8,12},{12,16},{16,20},{20,24},{24,28},{1,5},{5,9},{9,... | collective-permute-start | bytes 12296 | tf_op jit(solution)/shard_map/ppermute | solution.py:15
  82.8 33.2 %collective-permute-start = (f32[1,4,4,128]{3,2,1,0:T(4,128)S(1)}, f32[1,4,4,128]{3,2,1,0:T(4,128)S(1)}, u32[]{:S(2)}, u32[]{:S(2)}) collective-permute-start(f32[1,4,4,128]{3,2,1,0:T(4,128)S(1)} %fusion.28), channel_id=1, source_target_pairs={{1,0},{2,1},{3,2},{5,4},{6,5},{7,6},{9,8},{10,9},{11,10},{13,12},{... | collective-permute-start | bytes 24584 | tf_op jit(solution)/shard_map/ppermute | solution.py:18
  85.9 29.9 %copy-start.3 = (f32[4,4,384]{2,1,0:T(4,128)S(1)}, f32[4,4,384]{2,1,0:T(4,128)}, u32[]{:S(2)}) copy-start(f32[4,4,384]{2,1,0:T(4,128)} %param.15) | copy-start | bytes 73732
  86.0 30.0 %copy-start.7 = (s32[4,384]{1,0:T(4,128)S(1)}, s32[4,384]{1,0:T(4,128)}, u32[]{:S(2)}) copy-start(s32[4,384]{1,0:T(4,128)} %param.17) | copy-start | bytes 18436
  112.5 4.1 %collective-permute-start.1 = (f32[1,4,4,128]{3,2,1,0:T(4,128)S(1)}, f32[1,4,4,128]{3,2,1,0:T(4,128)S(1)}, u32[]{:S(2)}, u32[]{:S(2)}) collective-permute-start(f32[1,4,4,128]{3,2,1,0:T(4,128)S(1)} %fusion.27), channel_id=1, source_target_pairs={{0,1},{1,2},{2,3},{4,5},{5,6},{6,7},{8,9},{9,10},{10,11},{12,13},{... | collective-permute-start | bytes 24584 | tf_op jit(solution)/shard_map/ppermute | solution.py:15
  119.1 61.5 %collective-permute-start.6 = (f32[1,2,4,128]{3,2,1,0:T(4,128)S(1)}, f32[1,2,4,128]{3,2,1,0:T(4,128)S(1)}, u32[]{:S(2)}, u32[]{:S(2)}) collective-permute-start(f32[1,2,4,128]{3,2,1,0:T(4,128)S(1)} %select_bitcast_fusion.5), channel_id=1, source_target_pairs={{4,0},{8,4},{12,8},{16,12},{20,16},{24,20},{28,24},{5,1},{9,5},{13... | collective-permute-start | bytes 12296 | tf_op jit(solution)/shard_map/ppermute | solution.py:18
  120.4 60.4 %copy-start.2 = (f32[4,8,384]{2,1,0:T(8,128)S(1)}, f32[4,8,384]{2,1,0:T(8,128)}, u32[]{:S(2)}) copy-start(f32[4,8,384]{2,1,0:T(8,128)} %param.20) | copy-start | bytes 147460
  120.6 60.5 %copy-start.1 = (f32[4,24,384]{2,1,0:T(8,128)S(1)}, f32[4,24,384]{2,1,0:T(8,128)}, u32[]{:S(2)}) copy-start(f32[4,24,384]{2,1,0:T(8,128)} %param.19) | copy-start | bytes 442372
  122.6 97.7 %copy-start.5 = (f32[32,128]{1,0:T(8,128)S(1)}, f32[32,128]{1,0:T(8,128)}, u32[]{:S(2)}) copy-start(f32[32,128]{1,0:T(8,128)} %param.23) | copy-start | bytes 49156
  122.6 98.0 %copy-start.4 = (f32[1,96,384]{2,1,0:T(8,128)S(1)}, f32[1,96,384]{2,1,0:T(8,128)}, u32[]{:S(2)}) copy-start(f32[1,96,384]{2,1,0:T(8,128)} %param.22) | copy-start | bytes 442372
  122.6 58.0 %collective-permute-start.7 = (f32[1,2,4,128]{3,2,1,0:T(4,128)S(1)}, f32[1,2,4,128]{3,2,1,0:T(4,128)S(1)}, u32[]{:S(2)}, u32[]{:S(2)}) collective-permute-start(f32[1,2,4,128]{3,2,1,0:T(4,128)S(1)} %select_bitcast_fusion.4), channel_id=1, source_target_pairs={{0,4},{4,8},{8,12},{12,16},{16,20},{20,24},{24,28},{1,5},{5,9},{9,... | collective-permute-start | bytes 12296 | tf_op jit(solution)/shard_map/ppermute | solution.py:15
  131.0 49.7 %collective-permute-start.4 = (f32[1,4,4,128]{3,2,1,0:T(4,128)S(1)}, f32[1,4,4,128]{3,2,1,0:T(4,128)S(1)}, u32[]{:S(2)}, u32[]{:S(2)}) collective-permute-start(f32[1,4,4,128]{3,2,1,0:T(4,128)S(1)} %fusion.26), channel_id=1, source_target_pairs={{1,0},{2,1},{3,2},{5,4},{6,5},{7,6},{9,8},{10,9},{11,10},{13,12},{... | collective-permute-start | bytes 24584 | tf_op jit(solution)/shard_map/ppermute | solution.py:18
  137.3 43.4 %collective-permute-start.5 = (f32[1,4,4,128]{3,2,1,0:T(4,128)S(1)}, f32[1,4,4,128]{3,2,1,0:T(4,128)S(1)}, u32[]{:S(2)}, u32[]{:S(2)}) collective-permute-start(f32[1,4,4,128]{3,2,1,0:T(4,128)S(1)} %fusion.25), channel_id=1, source_target_pairs={{0,1},{1,2},{2,3},{4,5},{5,6},{6,7},{8,9},{9,10},{10,11},{12,13},{... | collective-permute-start | bytes 24584 | tf_op jit(solution)/shard_map/ppermute | solution.py:15
  231.6 21.7 %collective-permute-start.10 = (f32[1,2,4,128]{3,2,1,0:T(4,128)S(1)}, f32[1,2,4,128]{3,2,1,0:T(4,128)S(1)}, u32[]{:S(2)}, u32[]{:S(2)}) collective-permute-start(f32[1,2,4,128]{3,2,1,0:T(4,128)S(1)} %select_bitcast_fusion.3), channel_id=1, source_target_pairs={{4,0},{8,4},{12,8},{16,12},{20,16},{24,20},{28,24},{5,1},{9,5},{13... | collective-permute-start | bytes 12296 | tf_op jit(solution)/shard_map/ppermute | solution.py:18
  235.0 18.3 %collective-permute-start.11 = (f32[1,2,4,128]{3,2,1,0:T(4,128)S(1)}, f32[1,2,4,128]{3,2,1,0:T(4,128)S(1)}, u32[]{:S(2)}, u32[]{:S(2)}) collective-permute-start(f32[1,2,4,128]{3,2,1,0:T(4,128)S(1)} %select_bitcast_fusion.2), channel_id=1, source_target_pairs={{0,4},{4,8},{8,12},{12,16},{16,20},{20,24},{24,28},{1,5},{5,9},{9,... | collective-permute-start | bytes 12296 | tf_op jit(solution)/shard_map/ppermute | solution.py:15
  243.1 10.3 %collective-permute-start.8 = (f32[1,4,4,128]{3,2,1,0:T(4,128)S(1)}, f32[1,4,4,128]{3,2,1,0:T(4,128)S(1)}, u32[]{:S(2)}, u32[]{:S(2)}) collective-permute-start(f32[1,4,4,128]{3,2,1,0:T(4,128)S(1)} %fusion.24), channel_id=1, source_target_pairs={{1,0},{2,1},{3,2},{5,4},{6,5},{7,6},{9,8},{10,9},{11,10},{13,12},{... | collective-permute-start | bytes 24584 | tf_op jit(solution)/shard_map/ppermute | solution.py:18
  250.7 3.4 %collective-permute-start.9 = (f32[1,4,4,128]{3,2,1,0:T(4,128)S(1)}, f32[1,4,4,128]{3,2,1,0:T(4,128)S(1)}, u32[]{:S(2)}, u32[]{:S(2)}) collective-permute-start(f32[1,4,4,128]{3,2,1,0:T(4,128)S(1)} %fusion.23), channel_id=1, source_target_pairs={{0,1},{1,2},{2,3},{4,5},{5,6},{6,7},{8,9},{9,10},{10,11},{12,13},{... | collective-permute-start | bytes 24584 | tf_op jit(solution)/shard_map/ppermute | solution.py:15
  297.8 23.3 %collective-permute-start.14 = (f32[1,2,4,128]{3,2,1,0:T(4,128)S(1)}, f32[1,2,4,128]{3,2,1,0:T(4,128)S(1)}, u32[]{:S(2)}, u32[]{:S(2)}) collective-permute-start(f32[1,2,4,128]{3,2,1,0:T(4,128)S(1)} %select_bitcast_fusion.1), channel_id=1, source_target_pairs={{4,0},{8,4},{12,8},{16,12},{20,16},{24,20},{28,24},{5,1},{9,5},{13... | collective-permute-start | bytes 12296 | tf_op jit(solution)/shard_map/ppermute | solution.py:18
  301.4 19.7 %collective-permute-start.15 = (f32[1,2,4,128]{3,2,1,0:T(4,128)S(1)}, f32[1,2,4,128]{3,2,1,0:T(4,128)S(1)}, u32[]{:S(2)}, u32[]{:S(2)}) collective-permute-start(f32[1,2,4,128]{3,2,1,0:T(4,128)S(1)} %select_bitcast_fusion), channel_id=1, source_target_pairs={{0,4},{4,8},{8,12},{12,16},{16,20},{20,24},{24,28},{1,5},{5,9},{9,... | collective-permute-start | bytes 12296 | tf_op jit(solution)/shard_map/ppermute | solution.py:15
  309.4 11.8 %collective-permute-start.12 = (f32[1,4,4,128]{3,2,1,0:T(4,128)S(1)}, f32[1,4,4,128]{3,2,1,0:T(4,128)S(1)}, u32[]{:S(2)}, u32[]{:S(2)}) collective-permute-start(f32[1,4,4,128]{3,2,1,0:T(4,128)S(1)} %fusion.22), channel_id=1, source_target_pairs={{1,0},{2,1},{3,2},{5,4},{6,5},{7,6},{9,8},{10,9},{11,10},{13,12},{... | collective-permute-start | bytes 24584 | tf_op jit(solution)/shard_map/ppermute | solution.py:18
  317.5 4.3 %collective-permute-start.13 = (f32[1,4,4,128]{3,2,1,0:T(4,128)S(1)}, f32[1,4,4,128]{3,2,1,0:T(4,128)S(1)}, u32[]{:S(2)}, u32[]{:S(2)}) collective-permute-start(f32[1,4,4,128]{3,2,1,0:T(4,128)S(1)} %fusion.21), channel_id=1, source_target_pairs={{0,1},{1,2},{2,3},{4,5},{5,6},{6,7},{8,9},{9,10},{10,11},{12,13},{... | collective-permute-start | bytes 24584 | tf_op jit(solution)/shard_map/ppermute | solution.py:15
where the time goes:
time: 324 us; the launch traced here: 323 us
  blocking collectives  174 us (54%)
  local copies, waits for them, and re-layouts  86 us (27%)
  starting transfers between devices  48.9 us (15%)
  matrix products  9.13 us (3%)
    psum x3, blocking collectives, project(): lax.psum((corner_local, squares), ('cluster', 'sub'))  118 us
    gather x32, local copies, waits for them, and re-layouts, permuted(): return jnp.take_along_axis(blocks, order[:, None, :], axis=2)  46 us
    psum x1, blocking collectives, apply(): lax.psum(jnp.sum(spread * product, axis=(0, 2)), ('cluster', 'sub'))  41.2 us
    scatter x2, local copies, waits for them, and re-layouts, invert(): return jnp.zeros_like(order).at[row_index, order].set(col_index)  34 us
    ppermute x8, starting transfers between devices, extended(): lax.ppermute(lax.slice_in_dim(block, block.shape[dim] - width, None, axis...  30.2 us
    ppermute x8, starting transfers between devices, extended(): lax.ppermute(lax.slice_in_dim(block, 0, width, axis=dim), axis, backward)  18.7 us
    psum x2, blocking collectives, project(): cluster_all, global_all = lax.psum((part_cluster, part_global), 'sub')  14.4 us
  transfers between devices with their start and end apart: 16, of which 3 were waited for; matrix products, arithmetic and copies ran while one was open for 23% of the time, Pallas kernels for 0%

commit v1 on v0

--- a/solution.py
+++ b/solution.py
@@ -51,7 +51,8 @@
     product = jnp.einsum(
         "srk,skl->srl", spread.astype(jnp.bfloat16), operators, preferred_element_type=jnp.float32
     )
-    curvature = lax.psum(jnp.sum(spread * product, axis=(0, 2)), ("cluster", "sub"))
+    half = lax.psum(jnp.sum(spread * product, axis=(0, 2)), "sub")
+    curvature = lax.psum(half, "cluster")
     signed = sign_field * product
     result = signed + interface(signed, tables)
     return (result, curvature)

time: 324 us -> 292 us (0.901)
  blocking collectives: 174 us -> 136 us
  starting transfers between devices: 48.9 us -> 54.2 us
    psum x3 -> x2, blocking collectives: 118 us -> 77.7 us  [project(): lax.psum((corner_local, squares), ('cluster', 'sub'))]
    ppermute x8, starting transfers between devices: 18.7 us -> 24.4 us  [extended(): lax.ppermute(lax.slice_in_dim(block, 0, width, axis=dim), axis, backward)]
    psum x1 -> x4, blocking collectives: 41.2 us -> 43.5 us  [the longest x2 31.4 us: apply(): curvature = lax.psum(half, 'cluster')]
  transfers between devices with their start and end apart: 16 -> 16, of which waited for: 3 -> 4; matrix products, arithmetic and copies ran while one was open for 23% -> 25% of each run, Pallas kernels for 0% -> 0%
where the time goes in v1:
time: 292 us; the launch traced here: 291 us
  blocking collectives  136 us (47%)
  local copies, waits for them, and re-layouts  86 us (29%)
  starting transfers between devices  54.2 us (19%)
  matrix products  9.14 us (3%)
    psum x2, blocking collectives, project(): lax.psum((corner_local, squares), ('cluster', 'sub'))  77.7 us
    gather x32, local copies, waits for them, and re-layouts, permuted(): return jnp.take_along_axis(blocks, order[:, None, :], axis=2)  46 us
    scatter x2, local copies, waits for them, and re-layouts, invert(): return jnp.zeros_like(order).at[row_index, order].set(col_index)  34 us
    psum x2, blocking collectives, apply(): curvature = lax.psum(half, 'cluster')  31.4 us
    ppermute x8, starting transfers between devices, extended(): lax.ppermute(lax.slice_in_dim(block, block.shape[dim] - width, None, axis...  29.8 us
    ppermute x8, starting transfers between devices, extended(): lax.ppermute(lax.slice_in_dim(block, 0, width, axis=dim), axis, backward)  24.4 us
    psum x2, blocking collectives, project(): cluster_all, global_all = lax.psum((part_cluster, part_global), 'sub')  14.4 us
    psum x2, blocking collectives, apply(): half = lax.psum(jnp.sum(spread * product, axis=(0, 2)), 'sub')  12.1 us
  transfers between devices with their start and end apart: 16, of which 4 were waited for; matrix products, arithmetic and copies ran while one was open for 25% of the time, Pallas kernels for 0%

profile of v1, /device:TPU:1, one launch (start us, length us, event | category | flops | bytes accessed | tf_op | source)
XLA Modules:
  0.0 291.3 jit_solution(18262869369293428800)
XLA Ops:
  0.7 0.9 eq.15
  1.5 0.7 slice.78
  2.3 0.9 multiply_reduce_fusion.3
  3.1 1.2 convolution_bitcast_fusion.3
  4.5 1.0 convolution_bitcast_fusion.2
  5.8 1.1 fusion.3
  6.9 40.5 %all-reduce.1 = (f32[4,128]{1,0:T(4,128)S(1)}, f32[4]{0:T(128)S(1)}) all-reduce(f32[4,128]{1,0:T(4,128)S(1)} %fusion.16, f32[4]{0:T(128)S(1)} %multiply_reduce_fusion.3), channel_id=1, replica_groups=mesh['cluster'=8,'sub'=4] {'cluster','sub'}, use_global_device_ids=true, to_apply=%region_3.0 | all-reduce | flops 516 | bytes 4128 | tf_op jit(solution)/shard_map/psum | solution.py:74
  47.4 0.9 fusion.46
  48.3 7.2 %all-reduce.3 = (f32[4,384]{1,0:T(4,128)S(1)}, f32[4,128]{1,0:T(4,128)S(1)}) all-reduce(f32[4,384]{1,0:T(4,128)S(1)} %fusion.3, f32[4,128]{1,0:T(4,128)S(1)} %fusion.46), channel_id=1, replica_groups=mesh['cluster'=8,'sub'=4] {'sub'}, use_global_device_ids=true, to_apply=%region_2.0 | all-reduce | flops 2048 | bytes 16384 | tf_op jit(solution)/shard_map/psum | solution.py:79
  55.6 1.1 convolution_subtract_fusion.3
  56.9 0.6 gather_fusion
  57.5 1.1 convolution_subtract_fusion.2
  58.7 1.9 gather_fusion.3
  60.7 1.3 collective-permute-start.2
  62.1 11.4 %scatter_fusion.1 = s32[2,128]{1,0:T(2,128)S(1)} fusion(s32[2,128]{1,0:T(2,128)S(1)} %broadcast.105, s32[256]{0:T(256)S(1)} %fusion.53, s32[256]{0:T(256)S(1)} %iota_bitcast_fusion.1), kind=kCustom, calls=%fused_computation.19 | custom fusion | bytes 5120 | tf_op jit(solution)/shard_map/scatter | solution.py:26
  73.7 1.9 gather_fusion.4
  75.7 4.0 %collective-permute-start.3 = (f32[1,2,4,128]{3,2,1,0:T(4,128)S(1)}, f32[1,2,4,128]{3,2,1,0:T(4,128)S(1)}, u32[]{:S(2)}, u32[]{:S(2)}) collective-permute-start(f32[1,2,4,128]{3,2,1,0:T(4,128)S(1)} %select_bitcast_fusion.6), channel_id=1, source_target_pairs={{0,4},{4,8},{8,12},{12,16},{16,20},{20,24},{24,28},{1,5},{5,9},{9,... | collective-permute-start | bytes 12296 | tf_op jit(solution)/shard_map/ppermute | solution.py:15
  79.9 3.7 %gather_fusion.1 = f32[512,4]{1,0:T(8,128)S(1)} fusion(f32[4,4,128]{1,2,0:T(8,128)S(1)} %copy.49, s32[512]{0:T(512)S(1)} %get-tuple-element.39), kind=kCustom, calls=%fused_computation.1.clone | custom fusion | bytes 20480 | tf_op jit(solution)/shard_map/jit(take_along_axis)/gather | solution.py:30
  83.7 3.1 %collective-permute-start = (f32[1,4,4,128]{3,2,1,0:T(4,128)S(1)}, f32[1,4,4,128]{3,2,1,0:T(4,128)S(1)}, u32[]{:S(2)}, u32[]{:S(2)}) collective-permute-start(f32[1,4,4,128]{3,2,1,0:T(4,128)S(1)} %fusion.28), channel_id=1, source_target_pairs={{1,0},{2,1},{3,2},{5,4},{6,5},{7,6},{9,8},{10,9},{11,10},{13,12},{... | collective-permute-start | bytes 24584 | tf_op jit(solution)/shard_map/ppermute | solution.py:18
  86.8 22.5 %scatter_fusion = s32[4,128]{1,0:T(4,128)S(1)} fusion(s32[4,128]{1,0:T(4,128)S(1)} %broadcast.103, s32[512]{0:T(512)S(1)} %get-tuple-element.40, s32[512]{0:T(512)S(1)} %iota_bitcast_fusion), kind=kCustom, calls=%fused_computation.18 | custom fusion | bytes 10240 | tf_op jit(solution)/shard_map/scatter | solution.py:26
  109.5 3.7 %gather_fusion.2 = f32[512,4]{1,0:T(8,128)S(1)} fusion(f32[4,4,128]{1,2,0:T(8,128)S(1)} %copy.51, s32[512]{0:T(512)S(1)} %fusion.40), kind=kCustom, calls=%fused_computation.4.clone | custom fusion | bytes 20480 | tf_op jit(solution)/shard_map/jit(take_along_axis)/gather | solution.py:30
  113.3 3.3 %collective-permute-start.1 = (f32[1,4,4,128]{3,2,1,0:T(4,128)S(1)}, f32[1,4,4,128]{3,2,1,0:T(4,128)S(1)}, u32[]{:S(2)}, u32[]{:S(2)}) collective-permute-start(f32[1,4,4,128]{3,2,1,0:T(4,128)S(1)} %fusion.27), channel_id=1, source_target_pairs={{0,1},{1,2},{2,3},{4,5},{5,6},{6,7},{8,9},{9,10},{10,11},{12,13},{... | collective-permute-start | bytes 24584 | tf_op jit(solution)/shard_map/ppermute | solution.py:15
  116.7 0.7 collective-permute-done.1
  117.4 0.4 multiply_reduce_fusion.2
  117.8 6.1 %psum.88 = f32[4]{0:T(128)S(1)} all-reduce(f32[4]{0:T(128)S(1)} %get-tuple-element.17), channel_id=1, replica_groups=mesh['cluster'=8,'sub'=4] {'sub'}, use_global_device_ids=true, to_apply=%region_8.12 | all-reduce | flops 4 | bytes 32 | tf_op jit(solution)/shard_map/psum | solution.py:54
  123.9 15.6 %psum.89 = f32[4]{0:T(128)S(1)} all-reduce(f32[4]{0:T(128)S(1)} %psum.88), channel_id=1, replica_groups=mesh['cluster'=8,'sub'=4] {'cluster'}, use_global_device_ids=true, to_apply=%region_9.0 | all-reduce | flops 4 | bytes 32 | tf_op jit(solution)/shard_map/psum | solution.py:55
  139.7 1.9 gather_fusion.7
  141.7 1.3 collective-permute-start.6
  143.1 1.9 gather_fusion.8
  145.1 4.3 %collective-permute-start.7 = (f32[1,2,4,128]{3,2,1,0:T(4,128)S(1)}, f32[1,2,4,128]{3,2,1,0:T(4,128)S(1)}, u32[]{:S(2)}, u32[]{:S(2)}) collective-permute-start(f32[1,2,4,128]{3,2,1,0:T(4,128)S(1)} %select_bitcast_fusion.4), channel_id=1, source_target_pairs={{0,4},{4,8},{8,12},{12,16},{16,20},{20,24},{24,28},{1,5},{5,9},{9,... | collective-permute-start | bytes 12296 | tf_op jit(solution)/shard_map/ppermute | solution.py:15
  149.6 3.7 %gather_fusion.5 = f32[512,4]{1,0:T(8,128)S(1)} fusion(f32[4,4,128]{1,2,0:T(8,128)S(1)} %copy.57, s32[512]{0:T(512)S(1)} %get-tuple-element.39), kind=kCustom, calls=%fused_computation.5.clone | custom fusion | bytes 20480 | tf_op jit(solution)/shard_map/jit(take_along_axis)/gather | solution.py:30
  153.4 6.0 %collective-permute-start.4 = (f32[1,4,4,128]{3,2,1,0:T(4,128)S(1)}, f32[1,4,4,128]{3,2,1,0:T(4,128)S(1)}, u32[]{:S(2)}, u32[]{:S(2)}) collective-permute-start(f32[1,4,4,128]{3,2,1,0:T(4,128)S(1)} %fusion.26), channel_id=1, source_target_pairs={{1,0},{2,1},{3,2},{5,4},{6,5},{7,6},{9,8},{10,9},{11,10},{13,12},{... | collective-permute-start | bytes 24584 | tf_op jit(solution)/shard_map/ppermute | solution.py:18
  159.5 3.7 %gather_fusion.6 = f32[512,4]{1,0:T(8,128)S(1)} fusion(f32[4,4,128]{1,2,0:T(8,128)S(1)} %copy.59, s32[512]{0:T(512)S(1)} %fusion.40), kind=kCustom, calls=%fused_computation.6.clone | custom fusion | bytes 20480 | tf_op jit(solution)/shard_map/jit(take_along_axis)/gather | solution.py:30
  163.3 3.6 %collective-permute-start.5 = (f32[1,4,4,128]{3,2,1,0:T(4,128)S(1)}, f32[1,4,4,128]{3,2,1,0:T(4,128)S(1)}, u32[]{:S(2)}, u32[]{:S(2)}) collective-permute-start(f32[1,4,4,128]{3,2,1,0:T(4,128)S(1)} %fusion.25), channel_id=1, source_target_pairs={{0,1},{1,2},{2,3},{4,5},{5,6},{6,7},{8,9},{9,10},{10,11},{12,13},{... | collective-permute-start | bytes 24584 | tf_op jit(solution)/shard_map/ppermute | solution.py:15
  167.0 0.7 collective-permute-done.5
  168.1 0.3 convolution_bitcast_fusion.1
  168.6 37.3 %all-reduce = (f32[4,128]{1,0:T(4,128)S(1)}, f32[4]{0:T(128)S(1)}) all-reduce(f32[4,128]{1,0:T(4,128)S(1)} %fusion.15, f32[4]{0:T(128)S(1)} %get-tuple-element.13), channel_id=1, replica_groups=mesh['cluster'=8,'sub'=4] {'cluster','sub'}, use_global_device_ids=true, to_apply=%region_13.17 | all-reduce | flops 516 | bytes 4128 | tf_op jit(solution)/shard_map/psum | solution.py:74
  206.2 0.2 fusion.1
  206.4 7.2 %all-reduce.2 = (f32[4,384]{1,0:T(4,128)S(1)}, f32[4,128]{1,0:T(4,128)S(1)}) all-reduce(f32[4,384]{1,0:T(4,128)S(1)} %fusion.1, f32[4,128]{1,0:T(4,128)S(1)} %fusion.44), channel_id=1, replica_groups=mesh['cluster'=8,'sub'=4] {'sub'}, use_global_device_ids=true, to_apply=%region_12.16 | all-reduce | flops 2048 | bytes 16384 | tf_op jit(solution)/shard_map/psum | solution.py:79
  213.8 0.2 convolution_subtract_fusion.1
  214.1 0.6 gather_fusion.9
  214.7 0.3 fusion
  215.2 1.9 gather_fusion.12
  217.2 1.3 collective-permute-start.10
  218.7 1.9 gather_fusion.13
  220.6 4.0 %collective-permute-start.11 = (f32[1,2,4,128]{3,2,1,0:T(4,128)S(1)}, f32[1,2,4,128]{3,2,1,0:T(4,128)S(1)}, u32[]{:S(2)}, u32[]{:S(2)}) collective-permute-start(f32[1,2,4,128]{3,2,1,0:T(4,128)S(1)} %select_bitcast_fusion.2), channel_id=1, source_target_pairs={{0,4},{4,8},{8,12},{12,16},{16,20},{20,24},{24,28},{1,5},{5,9},{9,... | collective-permute-start | bytes 12296 | tf_op jit(solution)/shard_map/ppermute | solution.py:15
  224.8 3.7 %gather_fusion.10 = f32[512,4]{1,0:T(8,128)S(1)} fusion(f32[4,4,128]{1,2,0:T(8,128)S(1)} %copy.71, s32[512]{0:T(512)S(1)} %get-tuple-element.39), kind=kCustom, calls=%fused_computation.7.clone | custom fusion | bytes 20480 | tf_op jit(solution)/shard_map/jit(take_along_axis)/gather | solution.py:30
  228.6 3.3 %collective-permute-start.8 = (f32[1,4,4,128]{3,2,1,0:T(4,128)S(1)}, f32[1,4,4,128]{3,2,1,0:T(4,128)S(1)}, u32[]{:S(2)}, u32[]{:S(2)}) collective-permute-start(f32[1,4,4,128]{3,2,1,0:T(4,128)S(1)} %fusion.24), channel_id=1, source_target_pairs={{1,0},{2,1},{3,2},{5,4},{6,5},{7,6},{9,8},{10,9},{11,10},{13,12},{... | collective-permute-start | bytes 24584 | tf_op jit(solution)/shard_map/ppermute | solution.py:18
  232.0 3.7 %gather_fusion.11 = f32[512,4]{1,0:T(8,128)S(1)} fusion(f32[4,4,128]{1,2,0:T(8,128)S(1)} %copy.73, s32[512]{0:T(512)S(1)} %fusion.40), kind=kCustom, calls=%fused_computation.8.clone | custom fusion | bytes 20480 | tf_op jit(solution)/shard_map/jit(take_along_axis)/gather | solution.py:30
  235.8 3.1 %collective-permute-start.9 = (f32[1,4,4,128]{3,2,1,0:T(4,128)S(1)}, f32[1,4,4,128]{3,2,1,0:T(4,128)S(1)}, u32[]{:S(2)}, u32[]{:S(2)}) collective-permute-start(f32[1,4,4,128]{3,2,1,0:T(4,128)S(1)} %fusion.23), channel_id=1, source_target_pairs={{0,1},{1,2},{2,3},{4,5},{5,6},{6,7},{8,9},{9,10},{10,11},{12,13},{... | collective-permute-start | bytes 24584 | tf_op jit(solution)/shard_map/ppermute | solution.py:15
  239.0 0.7 collective-permute-done.9
  239.7 0.4 broadcast_multiply_fusion
  240.1 6.1 %psum.94 = f32[4]{0:T(128)S(1)} all-reduce(f32[4]{0:T(128)S(1)} %get-tuple-element.16), channel_id=1, replica_groups=mesh['cluster'=8,'sub'=4] {'sub'}, use_global_device_ids=true, to_apply=%region_16.20 | all-reduce | flops 4 | bytes 32 | tf_op jit(solution)/shard_map/psum | solution.py:54
  246.2 15.8 %psum.95 = f32[4]{0:T(128)S(1)} all-reduce(f32[4]{0:T(128)S(1)} %psum.94), channel_id=1, replica_groups=mesh['cluster'=8,'sub'=4] {'cluster'}, use_global_device_ids=true, to_apply=%region_17.21 | all-reduce | flops 4 | bytes 32 | tf_op jit(solution)/shard_map/psum | solution.py:55
  262.2 1.9 gather_fusion.16
  264.2 1.5 collective-permute-start.14
  265.8 1.9 gather_fusion.17
  267.8 4.0 %collective-permute-start.15 = (f32[1,2,4,128]{3,2,1,0:T(4,128)S(1)}, f32[1,2,4,128]{3,2,1,0:T(4,128)S(1)}, u32[]{:S(2)}, u32[]{:S(2)}) collective-permute-start(f32[1,2,4,128]{3,2,1,0:T(4,128)S(1)} %select_bitcast_fusion), channel_id=1, source_target_pairs={{0,4},{4,8},{8,12},{12,16},{16,20},{20,24},{24,28},{1,5},{5,9},{9,... | collective-permute-start | bytes 12296 | tf_op jit(solution)/shard_map/ppermute | solution.py:15
  272.0 3.7 %gather_fusion.14 = f32[512,4]{1,0:T(8,128)S(1)} fusion(f32[4,4,128]{1,2,0:T(8,128)S(1)} %copy.79, s32[512]{0:T(512)S(1)} %get-tuple-element.39), kind=kCustom, calls=%fused_computation.9.clone | custom fusion | bytes 20480 | tf_op jit(solution)/shard_map/jit(take_along_axis)/gather | solution.py:30
  275.8 6.7 %collective-permute-start.12 = (f32[1,4,4,128]{3,2,1,0:T(4,128)S(1)}, f32[1,4,4,128]{3,2,1,0:T(4,128)S(1)}, u32[]{:S(2)}, u32[]{:S(2)}) collective-permute-start(f32[1,4,4,128]{3,2,1,0:T(4,128)S(1)} %fusion.22), channel_id=1, source_target_pairs={{1,0},{2,1},{3,2},{5,4},{6,5},{7,6},{9,8},{10,9},{11,10},{13,12},{... | collective-permute-start | bytes 24584 | tf_op jit(solution)/shard_map/ppermute | solution.py:18
  282.6 3.7 %gather_fusion.15 = f32[512,4]{1,0:T(8,128)S(1)} fusion(f32[4,4,128]{1,2,0:T(8,128)S(1)} %copy.81, s32[512]{0:T(512)S(1)} %fusion.40), kind=kCustom, calls=%fused_computation.10.clone | custom fusion | bytes 20480 | tf_op jit(solution)/shard_map/jit(take_along_axis)/gather | solution.py:30
  286.4 3.4 %collective-permute-start.13 = (f32[1,4,4,128]{3,2,1,0:T(4,128)S(1)}, f32[1,4,4,128]{3,2,1,0:T(4,128)S(1)}, u32[]{:S(2)}, u32[]{:S(2)}) collective-permute-start(f32[1,4,4,128]{3,2,1,0:T(4,128)S(1)} %fusion.21), channel_id=1, source_target_pairs={{0,1},{1,2},{2,3},{4,5},{5,6},{6,7},{8,9},{9,10},{10,11},{12,13},{... | collective-permute-start | bytes 24584 | tf_op jit(solution)/shard_map/ppermute | solution.py:15
  289.9 0.7 collective-permute-done.13
  290.6 0.7 fusion.10
  (128 shorter events, 6.0 us)
Async XLA Ops:
  0.6 116.8 %copy-start = (bf16[4,384,384]{2,1,0:T(8,128)(2,1)S(1)}, bf16[4,384,384]{2,1,0:T(8,128)(2,1)}, u32[]{:S(2)}) copy-start(bf16[4,384,384]{2,1,0:T(8,128)(2,1)} %param.16) | copy-start | bytes 3538948
  0.6 61.4 %copy-start.6 = (s32[4,3,128]{2,0,1:T(4,128)S(1)}, s32[4,3,128]{2,0,1:T(4,128)}, u32[]{:S(2)}) copy-start(s32[4,3,128]{2,0,1:T(4,128)} %param.18) | copy-start | bytes 18436
  60.7 56.0 %collective-permute-start.2 = (f32[1,2,4,128]{3,2,1,0:T(4,128)S(1)}, f32[1,2,4,128]{3,2,1,0:T(4,128)S(1)}, u32[]{:S(2)}, u32[]{:S(2)}) collective-permute-start(f32[1,2,4,128]{3,2,1,0:T(4,128)S(1)} %select_bitcast_fusion.7), channel_id=1, source_target_pairs={{4,0},{8,4},{12,8},{16,12},{20,16},{24,20},{28,24},{5,1},{9,5},{13... | collective-permute-start | bytes 12296 | tf_op jit(solution)/shard_map/ppermute | solution.py:18
  75.7 41.0 %collective-permute-start.3 = (f32[1,2,4,128]{3,2,1,0:T(4,128)S(1)}, f32[1,2,4,128]{3,2,1,0:T(4,128)S(1)}, u32[]{:S(2)}, u32[]{:S(2)}) collective-permute-start(f32[1,2,4,128]{3,2,1,0:T(4,128)S(1)} %select_bitcast_fusion.6), channel_id=1, source_target_pairs={{0,4},{4,8},{8,12},{12,16},{16,20},{20,24},{24,28},{1,5},{5,9},{9,... | collective-permute-start | bytes 12296 | tf_op jit(solution)/shard_map/ppermute | solution.py:15
  83.7 33.0 %collective-permute-start = (f32[1,4,4,128]{3,2,1,0:T(4,128)S(1)}, f32[1,4,4,128]{3,2,1,0:T(4,128)S(1)}, u32[]{:S(2)}, u32[]{:S(2)}) collective-permute-start(f32[1,4,4,128]{3,2,1,0:T(4,128)S(1)} %fusion.28), channel_id=1, source_target_pairs={{1,0},{2,1},{3,2},{5,4},{6,5},{7,6},{9,8},{10,9},{11,10},{13,12},{... | collective-permute-start | bytes 24584 | tf_op jit(solution)/shard_map/ppermute | solution.py:18
  86.8 29.9 %copy-start.7 = (s32[4,384]{1,0:T(4,128)S(1)}, s32[4,384]{1,0:T(4,128)}, u32[]{:S(2)}) copy-start(s32[4,384]{1,0:T(4,128)} %param.17) | copy-start | bytes 18436
  113.3 4.1 %collective-permute-start.1 = (f32[1,4,4,128]{3,2,1,0:T(4,128)S(1)}, f32[1,4,4,128]{3,2,1,0:T(4,128)S(1)}, u32[]{:S(2)}, u32[]{:S(2)}) collective-permute-start(f32[1,4,4,128]{3,2,1,0:T(4,128)S(1)} %fusion.27), channel_id=1, source_target_pairs={{0,1},{1,2},{2,3},{4,5},{5,6},{6,7},{8,9},{9,10},{10,11},{12,13},{... | collective-permute-start | bytes 24584 | tf_op jit(solution)/shard_map/ppermute | solution.py:15
  141.6 26.1 %copy-start.3 = (f32[4,4,384]{2,1,0:T(4,128)S(1)}, f32[4,4,384]{2,1,0:T(4,128)}, u32[]{:S(2)}) copy-start(f32[4,4,384]{2,1,0:T(4,128)} %param.15) | copy-start | bytes 73732
  141.7 25.2 %collective-permute-start.6 = (f32[1,2,4,128]{3,2,1,0:T(4,128)S(1)}, f32[1,2,4,128]{3,2,1,0:T(4,128)S(1)}, u32[]{:S(2)}, u32[]{:S(2)}) collective-permute-start(f32[1,2,4,128]{3,2,1,0:T(4,128)S(1)} %select_bitcast_fusion.5), channel_id=1, source_target_pairs={{4,0},{8,4},{12,8},{16,12},{20,16},{24,20},{28,24},{5,1},{9,5},{13... | collective-permute-start | bytes 12296 | tf_op jit(solution)/shard_map/ppermute | solution.py:18
  143.0 24.9 %copy-start.2 = (f32[4,8,384]{2,1,0:T(8,128)S(1)}, f32[4,8,384]{2,1,0:T(8,128)}, u32[]{:S(2)}) copy-start(f32[4,8,384]{2,1,0:T(8,128)} %param.20) | copy-start | bytes 147460
  143.1 24.9 %copy-start.1 = (f32[4,24,384]{2,1,0:T(8,128)S(1)}, f32[4,24,384]{2,1,0:T(8,128)}, u32[]{:S(2)}) copy-start(f32[4,24,384]{2,1,0:T(8,128)} %param.19) | copy-start | bytes 442372
  145.0 60.9 %copy-start.5 = (f32[32,128]{1,0:T(8,128)S(1)}, f32[32,128]{1,0:T(8,128)}, u32[]{:S(2)}) copy-start(f32[32,128]{1,0:T(8,128)} %param.23) | copy-start | bytes 49156
  145.1 61.1 %copy-start.4 = (f32[1,96,384]{2,1,0:T(8,128)S(1)}, f32[1,96,384]{2,1,0:T(8,128)}, u32[]{:S(2)}) copy-start(f32[1,96,384]{2,1,0:T(8,128)} %param.22) | copy-start | bytes 442372
  145.1 21.8 %collective-permute-start.7 = (f32[1,2,4,128]{3,2,1,0:T(4,128)S(1)}, f32[1,2,4,128]{3,2,1,0:T(4,128)S(1)}, u32[]{:S(2)}, u32[]{:S(2)}) collective-permute-start(f32[1,2,4,128]{3,2,1,0:T(4,128)S(1)} %select_bitcast_fusion.4), channel_id=1, source_target_pairs={{0,4},{4,8},{8,12},{12,16},{16,20},{20,24},{24,28},{1,5},{5,9},{9,... | collective-permute-start | bytes 12296 | tf_op jit(solution)/shard_map/ppermute | solution.py:15
  153.4 13.6 %collective-permute-start.4 = (f32[1,4,4,128]{3,2,1,0:T(4,128)S(1)}, f32[1,4,4,128]{3,2,1,0:T(4,128)S(1)}, u32[]{:S(2)}, u32[]{:S(2)}) collective-permute-start(f32[1,4,4,128]{3,2,1,0:T(4,128)S(1)} %fusion.26), channel_id=1, source_target_pairs={{1,0},{2,1},{3,2},{5,4},{6,5},{7,6},{9,8},{10,9},{11,10},{13,12},{... | collective-permute-start | bytes 24584 | tf_op jit(solution)/shard_map/ppermute | solution.py:18
  163.3 4.4 %collective-permute-start.5 = (f32[1,4,4,128]{3,2,1,0:T(4,128)S(1)}, f32[1,4,4,128]{3,2,1,0:T(4,128)S(1)}, u32[]{:S(2)}, u32[]{:S(2)}) collective-permute-start(f32[1,4,4,128]{3,2,1,0:T(4,128)S(1)} %fusion.25), channel_id=1, source_target_pairs={{0,1},{1,2},{2,3},{4,5},{5,6},{6,7},{8,9},{9,10},{10,11},{12,13},{... | collective-permute-start | bytes 24584 | tf_op jit(solution)/shard_map/ppermute | solution.py:15
  217.2 21.7 %collective-permute-start.10 = (f32[1,2,4,128]{3,2,1,0:T(4,128)S(1)}, f32[1,2,4,128]{3,2,1,0:T(4,128)S(1)}, u32[]{:S(2)}, u32[]{:S(2)}) collective-permute-start(f32[1,2,4,128]{3,2,1,0:T(4,128)S(1)} %select_bitcast_fusion.3), channel_id=1, source_target_pairs={{4,0},{8,4},{12,8},{16,12},{20,16},{24,20},{28,24},{5,1},{9,5},{13... | collective-permute-start | bytes 12296 | tf_op jit(solution)/shard_map/ppermute | solution.py:18
  220.6 18.3 %collective-permute-start.11 = (f32[1,2,4,128]{3,2,1,0:T(4,128)S(1)}, f32[1,2,4,128]{3,2,1,0:T(4,128)S(1)}, u32[]{:S(2)}, u32[]{:S(2)}) collective-permute-start(f32[1,2,4,128]{3,2,1,0:T(4,128)S(1)} %select_bitcast_fusion.2), channel_id=1, source_target_pairs={{0,4},{4,8},{8,12},{12,16},{16,20},{20,24},{24,28},{1,5},{5,9},{9,... | collective-permute-start | bytes 12296 | tf_op jit(solution)/shard_map/ppermute | solution.py:15
  228.6 10.4 %collective-permute-start.8 = (f32[1,4,4,128]{3,2,1,0:T(4,128)S(1)}, f32[1,4,4,128]{3,2,1,0:T(4,128)S(1)}, u32[]{:S(2)}, u32[]{:S(2)}) collective-permute-start(f32[1,4,4,128]{3,2,1,0:T(4,128)S(1)} %fusion.24), channel_id=1, source_target_pairs={{1,0},{2,1},{3,2},{5,4},{6,5},{7,6},{9,8},{10,9},{11,10},{13,12},{... | collective-permute-start | bytes 24584 | tf_op jit(solution)/shard_map/ppermute | solution.py:18
  235.8 3.9 %collective-permute-start.9 = (f32[1,4,4,128]{3,2,1,0:T(4,128)S(1)}, f32[1,4,4,128]{3,2,1,0:T(4,128)S(1)}, u32[]{:S(2)}, u32[]{:S(2)}) collective-permute-start(f32[1,4,4,128]{3,2,1,0:T(4,128)S(1)} %fusion.23), channel_id=1, source_target_pairs={{0,1},{1,2},{2,3},{4,5},{5,6},{6,7},{8,9},{9,10},{10,11},{12,13},{... | collective-permute-start | bytes 24584 | tf_op jit(solution)/shard_map/ppermute | solution.py:15
  264.2 25.7 %collective-permute-start.14 = (f32[1,2,4,128]{3,2,1,0:T(4,128)S(1)}, f32[1,2,4,128]{3,2,1,0:T(4,128)S(1)}, u32[]{:S(2)}, u32[]{:S(2)}) collective-permute-start(f32[1,2,4,128]{3,2,1,0:T(4,128)S(1)} %select_bitcast_fusion.1), channel_id=1, source_target_pairs={{4,0},{8,4},{12,8},{16,12},{20,16},{24,20},{28,24},{5,1},{9,5},{13... | collective-permute-start | bytes 12296 | tf_op jit(solution)/shard_map/ppermute | solution.py:18
  267.8 22.0 %collective-permute-start.15 = (f32[1,2,4,128]{3,2,1,0:T(4,128)S(1)}, f32[1,2,4,128]{3,2,1,0:T(4,128)S(1)}, u32[]{:S(2)}, u32[]{:S(2)}) collective-permute-start(f32[1,2,4,128]{3,2,1,0:T(4,128)S(1)} %select_bitcast_fusion), channel_id=1, source_target_pairs={{0,4},{4,8},{8,12},{12,16},{16,20},{20,24},{24,28},{1,5},{5,9},{9,... | collective-permute-start | bytes 12296 | tf_op jit(solution)/shard_map/ppermute | solution.py:15
  275.8 14.1 %collective-permute-start.12 = (f32[1,4,4,128]{3,2,1,0:T(4,128)S(1)}, f32[1,4,4,128]{3,2,1,0:T(4,128)S(1)}, u32[]{:S(2)}, u32[]{:S(2)}) collective-permute-start(f32[1,4,4,128]{3,2,1,0:T(4,128)S(1)} %fusion.22), channel_id=1, source_target_pairs={{1,0},{2,1},{3,2},{5,4},{6,5},{7,6},{9,8},{10,9},{11,10},{13,12},{... | collective-permute-start | bytes 24584 | tf_op jit(solution)/shard_map/ppermute | solution.py:18
  286.4 4.2 %collective-permute-start.13 = (f32[1,4,4,128]{3,2,1,0:T(4,128)S(1)}, f32[1,4,4,128]{3,2,1,0:T(4,128)S(1)}, u32[]{:S(2)}, u32[]{:S(2)}) collective-permute-start(f32[1,4,4,128]{3,2,1,0:T(4,128)S(1)} %fusion.21), channel_id=1, source_target_pairs={{0,1},{1,2},{2,3},{4,5},{5,6},{6,7},{8,9},{9,10},{10,11},{12,13},{... | collective-permute-start | bytes 24584 | tf_op jit(solution)/shard_map/ppermute | solution.py:15
